TPU v7x, 512 devices: a whole 4x4x16 slice. The times are simulated.
512 devices in a mesh: row: 32 (over z, core), vec: 16 (over y, x).
Axes of the slice: x: 4, y: 4, z: 16, core: 2. Of those that a mesh axis runs over, the one named last changes fastest.
Arguments:
- vectors: float32 [32768, 2048], P('row', 'vec'), may hold values from -6 to 6
- reflectors: float32 [3, 32768, 512], P(None, ('row', 'vec')), may hold values from -0.03125 to 0.03125
- triangles: float32 [3, 512, 512], P(None, None, 'vec'), may hold values from -0.04 to 2, as said below
Outputs:
- transformed: float32 [32768, 2048], P('row', 'vec')
Inputs may be any that keep to these rules, and one draw needn't show every extreme that they name: Each triangles[k] is upper triangular with a diagonal between 0.5 and 2.
All inputs are finite; a program needn't handle non-finite values.
Results may differ from a plain program's by a relative error of at most 0.0001.
Values sent between devices are 32-bit elements; how exact they have to be, the bound alone decides.
A program may use at most 64 MiB of HBM per device.

v0:
```python
import jax
import jax.numpy as jnp
from jax import lax
from jax.sharding import Mesh
from jax.sharding import PartitionSpec as P

VEC = ("vec_0", "vec_1")
ROW_VEC = ("row", "vec_0", "vec_1")


def whole_of(x, axes, dim):
    for axis in reversed(axes):
        x = lax.all_gather(x, axis, axis=dim, tiled=True)
    return x


def cut_along(x, dim, count):
    before, after = (x.shape[:dim], x.shape[dim + 1 :])
    return jnp.moveaxis(x.reshape(*before, count, -1, *after), dim, 0)


def summed_on_arrival(x, axis, dim):
    count = lax.axis_size(axis)
    blocks = lax.all_to_all(cut_along(x, dim, count), axis, 0, 0, tiled=True)
    return jnp.sum(blocks, axis=0)


def from_everyone(x, axis):
    count = lax.axis_size(axis)
    return lax.all_to_all(jnp.broadcast_to(x[None], (count, *x.shape)), axis, 0, 0, tiled=True)


def laid_out(blocks, dim):
    lengths = list(blocks.shape[1:])
    lengths[dim] *= blocks.shape[0]
    return jnp.moveaxis(blocks, 0, dim).reshape(lengths)


def collect(x, axis, dim):
    blocks = from_everyone(x, axis)
    return laid_out(blocks, dim)


def per_device(vectors, reflectors, triangles):
    highest = lax.Precision.HIGHEST
    panels = reflectors.shape[0]
    current = vectors
    sections = lax.all_gather(reflectors, VEC, axis=1, tiled=True)
    factors = whole_of(triangles, VEC, 2)
    for step in range(panels):
        panel = panels - 1 - step
        section = sections[panel]
        factor = factors[panel]
        partial_value = lax.dot_general(
            section,
            current,
            (((0,), (0,)), ((), ())),
            precision=highest,
            preferred_element_type=jnp.float32,
        )
        share = summed_on_arrival(partial_value, "row", 1)
        owned = jnp.dot(factor, share, precision=highest, preferred_element_type=jnp.float32)
        coefficients = collect(owned, "row", 1)
        current = current - jnp.dot(
            section, coefficients, precision=highest, preferred_element_type=jnp.float32
        )
    return current


def solution(mesh):
    finer = Mesh(mesh.devices.reshape(mesh.shape["row"], 4, 4), ("row", "vec_0", "vec_1"))
    placed = (P("row", VEC), P(None, ROW_VEC, None), P(None, None, VEC))
    return jax.shard_map(
        per_device, mesh=finer, in_specs=placed, out_specs=P("row", VEC), check_vma=False
    )
```

profile of v0, /device:TPU:1, one launch (start us, length us, event | category | flops | bytes accessed | tf_op | source)
XLA Modules:
  0.0 311.0 jit_solution(14054268650420613728)
XLA Ops:
  6.5 0.0 all-gather.3.cloned.1.call-start
  6.5 0.7 all-gather.3.cloned.1.call-update
  7.3 0.0 all-gather.5.cloned.1.call-start
  7.3 14.0 %all_gather.10 = f32[3,512,128]{1,2,0:T(8,128)} all-gather(f32[3,512,32]{1,2,0:T(8,128)} %param.5), channel_id=1, replica_groups=mesh['row'=32,'vec_0'=4,'vec_1'=4] {'vec_1'}, dimensions={2}, use_global_device_ids=true | all-gather | bytes 983040 | tf_op jit(solution)/shard_map/all_gather | solution.py:13
  21.3 0.0 all-gather.5.cloned.1.call-update
  21.3 1.2 copy.17
  22.6 0.1 dot_general.48
  22.7 0.0 copy-start
  22.7 69.4 %all-gather.3.cloned.1.call-done = f32[3,1024,512]{2,1,0:T(8,128)} async-done(((f32[3,64,512]{2,1,0:T(8,128)}), f32[3,1024,512]{2,1,0:T(8,128)}) %all-gather.3.cloned.1.call-update) | async-done | bytes 6291472 | tf_op jit(solution)/shard_map/all_gather | solution.py:48
  92.1 3.1 fusion.22
  95.2 0.2 copy.19
  95.4 35.2 %all_to_all.30 = f32[32,512,4]{1,2,0:T(4,128)S(1)} all-to-all(f32[32,512,4]{1,2,0:T(4,128)S(1)} %copy.19), channel_id=1, replica_groups=mesh['row'=32,'vec_0'=4,'vec_1'=4] {'row'}, dimensions={0} | all-to-all | bytes 524288 | tf_op jit(solution)/shard_map/all_to_all | solution.py:24
  130.6 0.1 reduce_sum.27
  130.7 10.5 %all-gather.5.cloned.1.call-done = f32[3,512,512]{1,2,0:T(8,128)} async-done(((f32[3,512,128]{1,2,0:T(8,128)}), f32[3,512,512]{1,2,0:T(8,128)}) %all-gather.5.cloned.1.call-update) | async-done | bytes 3145744 | tf_op jit(solution)/shard_map/all_gather | solution.py:13
  141.2 1.8 convolution_bitcast_fusion.2
  143.0 0.7 broadcast_in_dim.6
  143.8 13.2 %all-to-all-start.1 = ((f32[32,512,4]{1,2,0:T(4,128)}), f32[32,512,4]{1,2,0:T(4,128)S(1)}, u32[]{:S(2)}, u32[]{:S(2)}) async-start(f32[32,512,4]{1,2,0:T(4,128)} %broadcast_in_dim.6), calls=%async_computation.1 | async-start | bytes 524288 | tf_op jit(solution)/shard_map/all_to_all | solution.py:30
  156.9 0.0 copy-done
  157.0 0.2 copy.20
  157.2 22.0 %all-to-all-done.1 = f32[32,512,4]{1,2,0:T(4,128)S(1)} async-done(((f32[32,512,4]{1,2,0:T(4,128)}), f32[32,512,4]{1,2,0:T(4,128)S(1)}, u32[]{:S(2)}, u32[]{:S(2)}) %all-to-all-start.1) | async-done | bytes 262176 | tf_op jit(solution)/shard_map/all_to_all | solution.py:30
  179.2 0.1 reshape.20
  179.3 3.9 %fusion.15 = f32[1024,128]{0,1:T(8,128)S(1)} fusion(f32[1024,128]{0,1:T(8,128)S(1)} %copy.20, f32[512,128]{0,1:T(8,128)S(1)} %reshape.20, f32[3,1024,512]{2,1,0:T(8,128)} %all-gather.3.cloned.1.call-done), kind=kOutput, calls=%fused_computation.15 | convolution fusion | flops 805437440 | bytes 3407872 | tf_op jit(solution)/shard_map/dot_general | solution.py:64
  183.2 2.9 fusion.21
  186.1 0.1 reshape.21
  186.1 24.9 %all_to_all.31 = f32[32,512,4]{1,2,0:T(4,128)S(1)} all-to-all(f32[32,512,4]{1,2,0:T(4,128)S(1)} %bitcast.91), channel_id=1, replica_groups=mesh['row'=32,'vec_0'=4,'vec_1'=4] {'row'}, dimensions={0} | all-to-all | bytes 524288 | tf_op jit(solution)/shard_map/all_to_all | solution.py:24
  211.1 0.1 reduce_sum.28
  211.1 1.8 convolution_bitcast_fusion.1
  213.0 25.9 %all_to_all.32 = f32[32,512,4]{1,2,0:T(4,128)S(1)} all-to-all(f32[32,512,4]{1,2,0:T(4,128)S(1)} %broadcast_in_dim.7), channel_id=1, replica_groups=mesh['row'=32,'vec_0'=4,'vec_1'=4] {'row'}, dimensions={0} | all-to-all | bytes 524288 | tf_op jit(solution)/shard_map/all_to_all | solution.py:30
  238.9 0.1 reshape.22
  239.0 3.9 %fusion.18 = f32[1024,128]{0,1:T(8,128)S(1)} fusion(f32[1024,128]{0,1:T(8,128)S(1)} %fusion.15, f32[512,128]{0,1:T(8,128)S(1)} %reshape.22, f32[3,1024,512]{2,1,0:T(8,128)} %all-gather.3.cloned.1.call-done), kind=kOutput, calls=%fused_computation.16 | convolution fusion | flops 805437440 | bytes 3407872 | tf_op jit(solution)/shard_map/dot_general | solution.py:64
  242.9 2.9 fusion.20
  245.8 0.1 reshape.23
  245.8 25.6 %all_to_all.33 = f32[32,512,4]{1,2,0:T(4,128)S(1)} all-to-all(f32[32,512,4]{1,2,0:T(4,128)S(1)} %bitcast.93), channel_id=1, replica_groups=mesh['row'=32,'vec_0'=4,'vec_1'=4] {'row'}, dimensions={0} | all-to-all | bytes 524288 | tf_op jit(solution)/shard_map/all_to_all | solution.py:24
  271.5 0.1 reduce_sum.29
  271.5 1.8 convolution_bitcast_fusion
  273.4 25.8 %all_to_all.34 = f32[32,512,4]{1,2,0:T(4,128)S(1)} all-to-all(f32[32,512,4]{1,2,0:T(4,128)S(1)} %broadcast_in_dim.8), channel_id=1, replica_groups=mesh['row'=32,'vec_0'=4,'vec_1'=4] {'row'}, dimensions={0} | all-to-all | bytes 524288 | tf_op jit(solution)/shard_map/all_to_all | solution.py:30
  299.2 0.1 reshape.24
  299.3 3.9 %fusion.19 = f32[1024,128]{0,1:T(8,128)S(1)} fusion(f32[1024,128]{0,1:T(8,128)S(1)} %fusion.18, f32[512,128]{0,1:T(8,128)S(1)} %reshape.24, f32[3,1024,512]{2,1,0:T(8,128)} %all-gather.3.cloned.1.call-done), kind=kOutput, calls=%fused_computation.17 | convolution fusion | flops 805437440 | bytes 3407872 | tf_op jit(solution)/shard_map/dot_general | solution.py:64
  303.1 1.0 copy.21
  (2 shorter events, 0.1 us)
Async XLA Ops:
  6.5 85.6 %all-gather.3.cloned.1.call-start = ((), (), s32[]{:S(2)}) async-start(), calls=%async_computation.6 | async-start | bytes 6684672 | tf_op jit(solution)/shard_map/all_gather | solution.py:48
  7.3 133.9 %all-gather.5.cloned.1.call-start = ((), (), s32[]{:S(2)}) async-start(), calls=%async_computation.7 | async-start | bytes 3932160 | tf_op jit(solution)/shard_map/all_gather | solution.py:13
  22.7 134.2 %copy-start = (f32[1024,128]{1,0:T(8,128)S(1)}, f32[1024,128]{1,0:T(8,128)}, u32[]{:S(2)}) copy-start(f32[1024,128]{1,0:T(8,128)} %param.3) | copy-start | bytes 1572868
  143.8 35.4 %all-to-all-start.1 = ((f32[32,512,4]{1,2,0:T(4,128)}), f32[32,512,4]{1,2,0:T(4,128)S(1)}, u32[]{:S(2)}, u32[]{:S(2)}) async-start(f32[32,512,4]{1,2,0:T(4,128)} %broadcast_in_dim.6), calls=%async_computation.1 | async-start | bytes 524288 | tf_op jit(solution)/shard_map/all_to_all | solution.py:30
Sparse Core Ops, SparseCore 0:
  10.3 81.6 all-gather.2
  94.2 46.9 all-gather.4
where the time goes:
time: 312 us; the launch traced here: 311 us
  blocking collectives  151 us (48%)
  waiting for transfers between devices  103 us (33%)
  matrix products  25.9 us (8%)
  between operations  13.5 us (4%)
  starting transfers between devices  13.2 us (4%)
  local copies, waits for them, and re-layouts  3.99 us (1%)
    all_to_all x3, blocking collectives, summed_on_arrival(): blocks = lax.all_to_all(cut_along(x, dim, count), axis, 0, 0, tiled=True)  85.8 us
    all_gather x1, waiting for transfers between devices, per_device(): sections = lax.all_gather(reflectors, VEC, axis=1, tiled=True)  69.4 us
    all_to_all x2, blocking collectives, from_everyone(): lax.all_to_all(jnp.broadcast_to(x[None], (count, *x.shape)), axis, 0, 0,...  51.7 us
    all_to_all x1, waiting for transfers between devices, from_everyone(): lax.all_to_all(jnp.broadcast_to(x[None], (count, *x.shape)), axis, 0, 0,...  22 us
    all_gather x1, blocking collectives, whole_of(): x = lax.all_gather(x, axis, axis=dim, tiled=True)  14 us
    all_to_all x1, starting transfers between devices, from_everyone(): lax.all_to_all(jnp.broadcast_to(x[None], (count, *x.shape)), axis, 0, 0,...  13.2 us
    dot_general x3, matrix products, per_device(): jnp.dot(section, coefficients, precision=highest, preferred_element_type=...  11.6 us
    all_gather x1, waiting for transfers between devices, whole_of(): x = lax.all_gather(x, axis, axis=dim, tiled=True)  10.5 us
  transfers between devices with their start and end apart: 3, of which 3 were waited for; matrix products, arithmetic and copies ran while one was open for 2% of the time, Pallas kernels for 0%

commit v1 on v0

v1 whole, which is shorter than its diff:
```python
import functools

import jax
import jax.numpy as jnp
from jax import lax
from jax.experimental import pallas as pl
from jax.experimental.pallas import tpu as pltpu
from jax.sharding import Mesh
from jax.sharding import PartitionSpec as P

MESH = pl.DeviceIdType.MESH
VEC = ("y", "x")
ROW = ("z", "core")

SPANS = ((0, 40, 24), (40, 40, 16))
OFFSETS = (0, -1, 1, 2)


def halves(value):
    high = value.astype(jnp.bfloat16)
    low = (value - high.astype(jnp.float32)).astype(jnp.bfloat16)
    return high, low


def product(a, b, dims):
    (a_high, a_low), (b_high, b_low) = a, b
    dot = functools.partial(lax.dot_general, dimension_numbers=(dims, ((), ())), preferred_element_type=jnp.float32)
    return dot(a_high, b_high) + (dot(a_high, b_low) + dot(a_low, b_high))


def kernel(
    x_ref, own_ref, out_ref,
    blocks, other_t, v_high, v_low, t_high, t_low, partial_c, from_core, chip_sum, arrived, coefs,
    gather_send, gather_recv, core_send, core_recv, scatter_send, scatter_recv, spread_send, spread_recv,
):
    panels = own_ref.shape[0]
    rows = own_ref.shape[1] - 16
    z, core = lax.axis_index("z"), lax.axis_index("core")
    y, x = lax.axis_index("y"), lax.axis_index("x")
    depth = lax.axis_size("z")
    place = {"x": x, "y": y}
    me = y * 4 + x

    def step(axis, by):
        return lax.rem(place[axis] + by + 4, 4)

    barrier = pltpu.get_barrier_semaphore()
    for axis in ("x", "y"):
        for by in (1, -1):
            pl.semaphore_signal(barrier, inc=1, device_id={axis: step(axis, by)}, device_id_type=MESH)
    pl.semaphore_signal(barrier, inc=1, device_id={"core": 1 - core}, device_id_type=MESH)
    for by in range(1, depth):
        pl.semaphore_signal(barrier, inc=1, device_id={"z": lax.rem(z + by, depth)}, device_id_type=MESH)
    pl.semaphore_wait(barrier, 5 + depth - 1)

    def block_at(half, first, second):
        first_axis, second_axis = ("x", "y") if half == 0 else ("y", "x")
        at = {first_axis: step(first_axis, first), second_axis: step(second_axis, second)}
        return at["y"] * 4 + at["x"]

    def part_of(half, part):
        start, size, cut = SPANS[half]
        return {"all": (start, size), "plus": (start, cut), "minus": (start + cut, size - cut)}[part]

    def transfer(panel, half, which, part, first, second, second_leg, by, from_own=False):
        index = block_at(half, first, second)
        start, size = part_of(half, part)
        there = blocks.at[panel, index, pl.ds(start, size), :]
        here = own_ref.at[panel, pl.ds(start, size), :] if from_own else there
        axis = ("x", "y")[(half + second_leg) % 2]
        return pltpu.make_async_remote_copy(
            src_ref=here, dst_ref=there,
            send_sem=gather_send.at[panel, half * 20 + which], recv_sem=gather_recv.at[panel, half * 20 + which],
            device_id={axis: step(axis, by)}, device_id_type=MESH,
        )

    sent = []

    def send(*args, **kwargs):
        copy = transfer(*args, **kwargs)
        copy.start()
        sent.append(copy)

    def gather_0(p):
        for h in (0, 1):
            send(p, h, 0, "all", 0, 0, 0, 1, from_own=True)
            send(p, h, 1, "all", 0, 0, 0, -1, from_own=True)
        for h in (0, 1):
            send(p, h, 4, "all", 0, 0, 1, 1, from_own=True)
            send(p, h, 8, "all", 0, 0, 1, -1, from_own=True)
        blocks[p, me] = own_ref[p]

    def gather_1(p):
        for h in (0, 1):
            transfer(p, h, 0, "all", -1, 0, 0, 1).wait_recv()
            send(p, h, 2, "plus", -1, 0, 0, 1)
            transfer(p, h, 1, "all", 1, 0, 0, -1).wait_recv()
            send(p, h, 3, "minus", 1, 0, 0, -1)
        for h in (0, 1):
            for s in (1, 2):
                send(p, h, 4 + s, "all", OFFSETS[s], 0, 1, 1)
                send(p, h, 8 + s, "all", OFFSETS[s], 0, 1, -1)

    def gather_2(p):
        for h in (0, 1):
            transfer(p, h, 2, "plus", 2, 0, 0, 1).wait_recv()
            transfer(p, h, 3, "minus", 2, 0, 0, -1).wait_recv()
            send(p, h, 7, "all", 2, 0, 1, 1)
            send(p, h, 11, "all", 2, 0, 1, -1)

    def gather_3(p):
        for s in range(4):
            for h in (0, 1):
                transfer(p, h, 4 + s, "all", OFFSETS[s], -1, 1, 1).wait_recv()
                send(p, h, 12 + s, "plus", OFFSETS[s], -1, 1, 1)
                transfer(p, h, 8 + s, "all", OFFSETS[s], 1, 1, -1).wait_recv()
                send(p, h, 16 + s, "minus", OFFSETS[s], 1, 1, -1)

    def gather_4(p):
        for s in range(4):
            for h in (0, 1):
                transfer(p, h, 12 + s, "plus", OFFSETS[s], 2, 1, 1).wait_recv()
                transfer(p, h, 16 + s, "minus", OFFSETS[s], 2, 1, -1).wait_recv()

    def to_core(src, dst, which):
        return pltpu.make_async_remote_copy(
            src_ref=src, dst_ref=dst, send_sem=core_send.at[which], recv_sem=core_recv.at[which],
            device_id={"core": 1 - core}, device_id_type=MESH,
        )

    def start(copy):
        copy.start()
        sent.append(copy)

    def factor_copy(p):
        return to_core(blocks.at[p, :, pl.ds(rows, 16), :], other_t.at[p], p)

    def prepare(p):
        start(factor_copy(p))

        @pl.loop(0, 16)
        def _(b):
            high, low = halves(blocks[p, b, 0:rows, :])
            at = pl.ds(pl.multiple_of(b * rows, rows), rows)
            v_high[p, at, :] = high
            v_low[p, at, :] = low
            high, low = halves(blocks[p, b, rows:, :])
            at = pl.ds(pl.multiple_of(b * 32 + core * 16, 16), 16)
            t_high[p, at, :] = high
            t_low[p, at, :] = low

        factor_copy(p).wait_recv()

        @pl.loop(0, 16)
        def _(b):
            high, low = halves(other_t[p, b])
            at = pl.ds(pl.multiple_of(b * 32 + (1 - core) * 16, 16), 16)
            t_high[p, at, :] = high
            t_low[p, at, :] = low

    far_first = sorted(range(1, 16), key=lambda d: -min(d, 16 - d))

    def share_of(at):
        return pl.ds(pl.multiple_of(at // 2 * 8, 8), 8), pl.ds(pl.multiple_of(at % 2 * 256, 256), 256)

    def scatter_copy(p, by):
        to = lax.rem(z + by, depth)
        down, along = share_of(to)
        return pltpu.make_async_remote_copy(
            src_ref=chip_sum.at[p, down, along], dst_ref=arrived.at[p, by],
            send_sem=scatter_send.at[p, by], recv_sem=scatter_recv.at[p, by],
            device_id={"z": to}, device_id_type=MESH,
        )

    def spread_copy(p, by, of):
        down, along = share_of(of)
        at = coefs.at[p, core, down, along]
        return pltpu.make_async_remote_copy(
            src_ref=at, dst_ref=at,
            send_sem=spread_send.at[p, by], recv_sem=spread_recv.at[p, by],
            device_id={"z": lax.rem(z + by, depth)}, device_id_type=MESH,
        )

    def core_sum_copy(p):
        return to_core(partial_c.at[p, 1 - core], from_core.at[p], panels + p)

    def core_spread_copy(p, which):
        return to_core(coefs.at[p, which], coefs.at[p, which], 2 * panels + p)

    last = panels - 1
    gather_0(last)
    out_ref[...] = x_ref[...]
    gather_1(last)
    gather_2(last)
    gather_3(last)
    gather_0(last - 1)
    gather_4(last)
    prepare(last)
    for p in range(last, -1, -1):
        turned = halves(out_ref[...].T)
        projected = product(turned, (v_high[p], v_low[p]), ((1,), (0,)))
        value = product(halves(projected), (t_high[p], t_low[p]), ((1,), (0,)))
        half = value.shape[0] // 2
        partial_c[p, 0] = value[:half]
        partial_c[p, 1] = value[half:]
        start(core_sum_copy(p))
        if p > 0:
            gather_1(p - 1)
        core_sum_copy(p).wait_recv()
        chip_sum[p] = partial_c[p, core] + from_core[p]
        for by in far_first:
            start(scatter_copy(p, by))
        if p > 0:
            gather_2(p - 1)
        down, along = share_of(z)
        total = chip_sum[p, down, along]
        for by in range(1, 16):
            scatter_copy(p, by).wait_recv()
        for by in range(1, 16):
            total = total + arrived[p, by]
        coefs[p, core, down, along] = total
        for by in far_first:
            start(spread_copy(p, by, z))
        if p > 0:
            gather_3(p - 1)
            if p > 1:
                gather_0(p - 2)
            gather_4(p - 1)
            prepare(p - 1)
        for by in range(1, 16):
            spread_copy(p, by, lax.rem(z + depth - by, depth)).wait_recv()
        start(core_spread_copy(p, core))
        core_spread_copy(p, 1 - core).wait_recv()
        turned_c = halves(jnp.concatenate([coefs[p, 0], coefs[p, 1]], axis=0))
        out_ref[...] = out_ref[...] - product((v_high[p], v_low[p]), turned_c, ((1,), (1,)))
    for copy in sent:
        copy.wait_send()


def per_device(vectors, reflectors, triangles):
    panels, rows, width = reflectors.shape
    count = vectors.shape[1]
    everyone = 16 * rows
    turned = jnp.swapaxes(triangles, 1, 2)
    half = turned.shape[1] // 2
    mine = lax.dynamic_slice_in_dim(turned, lax.axis_index("core") * half, half, axis=1)
    own = jnp.concatenate([reflectors, mine], axis=1)
    f32, bf16 = jnp.float32, jnp.bfloat16
    dma = pltpu.SemaphoreType.DMA
    return pl.pallas_call(
        kernel,
        out_shape=jax.ShapeDtypeStruct(vectors.shape, f32),
        in_specs=[pl.BlockSpec(memory_space=pltpu.VMEM)] * 2,
        out_specs=pl.BlockSpec(memory_space=pltpu.VMEM),
        scratch_shapes=[
            pltpu.VMEM((panels, 16, rows + half, width), f32),
            pltpu.VMEM((panels, 16, half, width), f32),
            pltpu.VMEM((panels, everyone, width), bf16),
            pltpu.VMEM((panels, everyone, width), bf16),
            pltpu.VMEM((panels, width, width), bf16),
            pltpu.VMEM((panels, width, width), bf16),
            pltpu.VMEM((panels, 2, count // 2, width), f32),
            pltpu.VMEM((panels, count // 2, width), f32),
            pltpu.VMEM((panels, count // 2, width), f32),
            pltpu.VMEM((panels, 16, 8, 256), f32),
            pltpu.VMEM((panels, 2, count // 2, width), f32),
            dma((panels, 40)), dma((panels, 40)),
            dma((3 * panels,)), dma((3 * panels,)),
            dma((panels, 16)), dma((panels, 16)),
            dma((panels, 16)), dma((panels, 16)),
        ],
        compiler_params=pltpu.CompilerParams(collective_id=0, has_side_effects=True),
    )(vectors, own)


def solution(mesh):
    finer = Mesh(mesh.devices.reshape(16, 2, 4, 4), ("z", "core", "y", "x"))
    placed = (P(ROW, VEC), P(None, ROW + VEC, None), P(None, None, VEC))
    return jax.shard_map(
        per_device, mesh=finer, in_specs=placed, out_specs=P(ROW, VEC), check_vma=False
    )
```

time: 312 us -> 114 us (0.37)
  blocking collectives: 151 us -> 0 us
  Pallas kernels: 0 us -> 109 us
  waiting for transfers between devices: 103 us -> 0 us
  matrix products: 25.9 us -> 0 us
  between operations: 13.5 us -> 0.01 us
  starting transfers between devices: 13.2 us -> 0 us
    all_to_all x5 -> x0, blocking collectives: 137 us -> none  [the longest x3 85.8 us: summed_on_arrival(): blocks = lax.all_to_all(cut_along(x, dim, count), axis, 0, 0, tiled=True)]
    pallas_call x0 -> x1, Pallas kernels: none -> 109 us  [per_device(): pl.pallas_call(kernel, out_shape=jax.ShapeDtypeStruct(vectors.shape, f32)...]
    all_gather x2 -> x0, waiting for transfers between devices: 79.9 us -> none  [the longest x1 69.4 us: per_device(): sections = lax.all_gather(reflectors, VEC, axis=1, tiled=True)]
    dot_general x9 -> x0, matrix products: 25.9 us -> none  [the longest x3 11.6 us: per_device(): jnp.dot(section, coefficients, precision=highest, preferred_element_type=...]
    all_to_all x1 -> x0, waiting for transfers between devices: 22 us -> none  [from_everyone(): lax.all_to_all(jnp.broadcast_to(x[None], (count, *x.shape)), axis, 0, 0,...]
    all_gather x1 -> x0, blocking collectives: 14 us -> none  [whole_of(): x = lax.all_gather(x, axis, axis=dim, tiled=True)]
    all_to_all x1 -> x0, starting transfers between devices: 13.2 us -> none  [from_everyone(): lax.all_to_all(jnp.broadcast_to(x[None], (count, *x.shape)), axis, 0, 0,...]
  transfers between devices with their start and end apart: 3 -> 0, of which waited for: 3 -> 0; matrix products, arithmetic and copies ran while one was open for 2% -> 0% of each run, Pallas kernels for 0% -> 0%
where the time goes in v1:
time: 114 us
  Pallas kernels  109 us (96%)
  local copies, waits for them, and re-layouts  2.8 us (2%)
  other arithmetic  1.81 us (2%)
    pallas_call x1, Pallas kernels, per_device(): pl.pallas_call(kernel, out_shape=jax.ShapeDtypeStruct(vectors.shape, f32)...  109 us
    unnamed x3, local copies, waits for them, and re-layouts  2.8 us

profile of v1, /device:TPU:1, one launch (start us, length us, event | category | flops | bytes accessed | tf_op | source)
XLA Modules:
  0.0 113.6 jit_solution(18202125491881006908)
XLA Ops:
  0.0 0.0 copy-start
  0.0 0.9 copy-done
  0.9 1.8 %pad_maximum_fusion.own_ref = f32[3,80,512]{2,1,0:T(8,128)} fusion(f32[3,16,512]{2,1,0:T(8,128)S(1)} %dynamic-slice_bitcast_fusion, f32[3,64,512]{2,1,0:T(8,128)} %param.4), kind=kLoop, calls=%fused_computation | loop fusion | flops 122880 | bytes 983040 | tf_op jit(solution)/shard_map/concatenate | solution.py:247
  2.7 109.0 %shard_map.37 = f32[1024,128]{1,0:T(8,128)} custom-call(f32[1024,128]{1,0:T(8,128)} %x_ref.1, f32[3,80,512]{2,1,0:T(8,128)} %pad_maximum_fusion.own_ref), custom_call_target="tpu_custom_call" | custom-call | tf_op jit(solution)/shard_map/pallas_call | solution.py:250
  111.7 1.9 %copy.5 = f32[1024,128]{1,0:T(8,128)} copy(f32[1024,128]{1,0:T(8,128)} %shard_map.37) | data formatting | bytes 1048576
  (1 shorter events, 0.0 us)
Async XLA Ops:
  0.0 0.9 copy-start

commit v2 on v0

v2 whole, which is shorter than its diff:
```python
import functools

import jax
import jax.numpy as jnp
from jax import lax
from jax.experimental import pallas as pl
from jax.experimental.pallas import tpu as pltpu
from jax.sharding import Mesh
from jax.sharding import PartitionSpec as P

MESH = pl.DeviceIdType.MESH
VEC = ("y", "x")
ROW = ("z", "core")
STREAMS = 2

SPANS = ((0, 40, 24), (40, 40, 16))
OFFSETS = (0, -1, 1, 2)


def halves(value):
    high = value.astype(jnp.bfloat16)
    low = (value - high.astype(jnp.float32)).astype(jnp.bfloat16)
    return high, low


def product(a, b_high, b_low, contracted):
    a_high, a_low = halves(a)
    count = a.shape[0]
    dot = functools.partial(
        lax.dot_general, dimension_numbers=(((1,), (contracted,)), ((), ())), preferred_element_type=jnp.float32
    )
    both = dot(jnp.concatenate([a_high, a_low], axis=0), b_high)
    return both[:count] + (dot(a_high, b_low) + both[count:])


def kernel(
    x_ref, reflectors_ref, factors_ref, out_ref,
    x_in, x_turned, blocks, other_t, v_high, v_low, t_high, t_low, partial_c, near, near_sum, far, coefs,
    load_sem, entered, gather_send, gather_first, gather_opposite, gather_second, gather_last,
    core_send, factor_recv, near_send, near_recv, far_send, far_recv, spread_send, spread_recv,
):
    panels, rows, width = reflectors_ref.shape
    half_t = factors_ref.shape[1] // 2
    z, core = lax.axis_index("z"), lax.axis_index("core")
    y, x = lax.axis_index("y"), lax.axis_index("x")
    depth = lax.axis_size("z")
    place = {"x": x, "y": y}
    me = y * 4 + x
    last = panels - 1

    def scope(name):
        return jax.named_scope(name)

    def step(axis, by):
        return lax.rem(place[axis] + by + 4, 4)

    def up(by):
        return lax.rem(z + by + depth, depth)

    loads = []
    for p in range(last, -1, -1):
        loads.append(pltpu.make_async_copy(reflectors_ref.at[p], blocks.at[p, me, pl.ds(0, rows), :], load_sem.at[2 * p]))
        loads.append(
            pltpu.make_async_copy(
                factors_ref.at[p, pl.ds(pl.multiple_of(core * half_t, half_t), half_t), :],
                blocks.at[p, me, pl.ds(rows, half_t), :],
                load_sem.at[2 * p + 1],
            )
        )
    load_x = pltpu.make_async_copy(x_ref, x_in, load_sem.at[2 * panels])
    for copy in loads:
        copy.start()
    load_x.start()

    with scope("barrier"):
        barrier = pltpu.get_barrier_semaphore()
        for axis in ("x", "y"):
            for by in (1, -1):
                pl.semaphore_signal(barrier, inc=1, device_id={axis: step(axis, by)}, device_id_type=MESH)
        pl.semaphore_signal(barrier, inc=1, device_id={"core": 1 - core}, device_id_type=MESH)
        for by in (1, -1, 2, -2):
            for other in (core, 1 - core):
                pl.semaphore_signal(barrier, inc=1, device_id={"z": up(by), "core": other}, device_id_type=MESH)
        for copy in loads:
            copy.wait()
        pl.semaphore_wait(barrier, 13)

    def announce(round_):
        for by in (1, -1):
            pl.semaphore_signal(entered.at[round_], inc=1, device_id={"z": up(by * 2 * 2**round_)}, device_id_type=MESH)

    def heard(round_):
        pl.semaphore_wait(entered.at[round_], 2)

    def block_at(half, first, second):
        first_axis, second_axis = ("x", "y") if half == 0 else ("y", "x")
        at = {first_axis: step(first_axis, first), second_axis: step(second_axis, second)}
        return at["y"] * 4 + at["x"]

    def transfer(panel, half, recv, part, first, second, second_leg, by):
        start, size, cut = SPANS[half]
        start, size = {"all": (start, size), "plus": (start, cut), "minus": (start + cut, size - cut)}[part]
        there = blocks.at[panel, block_at(half, first, second), pl.ds(start, size), :]
        axis = ("x", "y")[(half + second_leg) % 2]
        return pltpu.make_async_remote_copy(
            src_ref=there, dst_ref=there, send_sem=gather_send.at[panel], recv_sem=recv,
            device_id={axis: step(axis, by)}, device_id_type=MESH,
        )

    def side(by):
        return 0 if by == 1 else 1

    def first_leg(p, h, by, first=0):
        return transfer(p, h, gather_first.at[p, 2 * h + side(by)], "all", first, 0, 0, by)

    def opposite(p, h, part, by, first):
        return transfer(p, h, gather_opposite.at[p, h], part, first, 0, 0, by)

    def second_leg(p, h, s, by, second=0):
        return transfer(p, h, gather_second.at[p, (h * 4 + s) * 2 + side(by)], "all", OFFSETS[s], second, 1, by)

    def final_leg(p, h, s, part, by):
        return transfer(p, h, gather_last.at[p], part, OFFSETS[s], -by, 1, by)

    def gather_0(p):
        for h in (0, 1):
            for by in (1, -1):
                first_leg(p, h, by).start()
        for h in (0, 1):
            for by in (1, -1):
                second_leg(p, h, 0, by).start()

    def gather_1(p):
        for h in (0, 1):
            first_leg(p, h, 1, -1).wait_recv()
            opposite(p, h, "plus", 1, -1).start()
            first_leg(p, h, -1, 1).wait_recv()
            opposite(p, h, "minus", -1, 1).start()
        for h in (0, 1):
            for s in (1, 2):
                for by in (1, -1):
                    second_leg(p, h, s, by).start()

    def gather_2(p):
        for h in (0, 1):
            opposite(p, h, "all", 1, 2).wait_recv()
            for by in (1, -1):
                second_leg(p, h, 3, by).start()

    def gather_3(p, which):
        for s in which:
            for h in (0, 1):
                for by, part in ((1, "plus"), (-1, "minus")):
                    second_leg(p, h, s, by, -by).wait_recv()
                    final_leg(p, h, s, part, by).start()

    def gather_4(p):
        whole = blocks.at[p, pl.ds(0, 4)]
        pltpu.make_async_remote_copy(
            src_ref=whole, dst_ref=whole, send_sem=gather_send.at[p], recv_sem=gather_last.at[p],
            device_id={"core": 1 - core}, device_id_type=MESH,
        ).wait_recv()

    def to_core(src, dst, send, recv):
        return pltpu.make_async_remote_copy(
            src_ref=src, dst_ref=dst, send_sem=core_send.at[send], recv_sem=recv,
            device_id={"core": 1 - core}, device_id_type=MESH,
        )

    def factor_copy(p):
        return to_core(blocks.at[p, :, pl.ds(rows, half_t), :], other_t.at[p], 0, factor_recv.at[p])

    def prepare(p):
        factor_copy(p).start()

        @pl.loop(0, 16)
        def _(b):
            at = pl.ds(pl.multiple_of(b * rows, rows), rows)
            v_high[p, at, :], v_low[p, at, :] = halves(blocks[p, b, 0:rows, :])
            at = pl.ds(pl.multiple_of(b * 32 + core * 16, 16), 16)
            t_high[p, at, :], t_low[p, at, :] = halves(blocks[p, b, rows:, :])

        factor_copy(p).wait_recv()

        @pl.loop(0, 16)
        def _(b):
            at = pl.ds(pl.multiple_of(b * 32 + (1 - core) * 16, 16), 16)
            t_high[p, at, :], t_low[p, at, :] = halves(other_t[p, b])

    count = x_turned.shape[0] // STREAMS
    NEAR = ((0, 1), (1, 0), (1, 1), (-1, 0), (-1, 1), (2, 0), (2, 1))

    def towards(s, by):
        return by if s % 2 == 0 else -by

    def part_of(chip, core_):
        return pl.ds(pl.multiple_of((lax.rem(chip, 4) * 2 + core_) * (count // 8), count // 8), count // 8)

    def near_copy(p, s, i):
        by, flip = NEAR[i]
        to, other = up(towards(s, by)), core + flip - 2 * core * flip
        return pltpu.make_async_remote_copy(
            src_ref=partial_c.at[p, s, part_of(to, other)], dst_ref=near.at[p, s, i],
            send_sem=near_send.at[0], recv_sem=near_recv.at[p, s],
            device_id={"z": to, "core": other}, device_id_type=MESH,
        )

    def far_copy(p, s, i):
        return pltpu.make_async_remote_copy(
            src_ref=near_sum.at[p, s], dst_ref=far.at[p, s, i],
            send_sem=far_send.at[0], recv_sem=far_recv.at[p, s],
            device_id={"z": up(4 * (i + 1))}, device_id_type=MESH,
        )

    def spread_copy(p, s, i):
        by, flip = NEAR[i]
        own = coefs.at[p, s, part_of(z, core)]
        return pltpu.make_async_remote_copy(
            src_ref=own, dst_ref=own, send_sem=spread_send.at[0], recv_sem=spread_recv.at[p, s],
            device_id={"z": up(-towards(s, by)), "core": core + flip - 2 * core * flip}, device_id_type=MESH,
        )

    def whole_of(ref, send, recv):
        return pltpu.make_async_remote_copy(
            src_ref=ref, dst_ref=ref, send_sem=send, recv_sem=recv, device_id={"core": 1 - core}, device_id_type=MESH
        )

    def columns(s):
        return slice(s * count, (s + 1) * count)

    def project(p, s):
        projected = product(x_turned[columns(s), :], v_high[p], v_low[p], 0)
        partial_c[p, s] = product(projected, t_high[p], t_low[p], 0)
        for i in (5, 6, 1, 2, 3, 4, 0):
            near_copy(p, s, i).start()

    def sum_near(p, s):
        whole_of(near.at[p, s], near_send.at[0], near_recv.at[p, s]).wait_recv()
        total = partial_c[p, s, part_of(z, core)]
        for i in range(7):
            total = total + near[p, s, i]
        near_sum[p, s] = total
        for i in (1, 0, 2):
            far_copy(p, s, i).start()

    def sum_far(p, s):
        whole_of(far.at[p, s], far_send.at[0], far_recv.at[p, s]).wait_recv()
        coefs[p, s, part_of(z, core)] = (near_sum[p, s] + far[p, s, 1]) + (far[p, s, 0] + far[p, s, 2])
        for i in (5, 6, 1, 2, 3, 4, 0):
            spread_copy(p, s, i).start()

    def update(p, s):
        whole_of(near.at[p, s], spread_send.at[0], spread_recv.at[p, s]).wait_recv()
        x_turned[columns(s), :] = x_turned[columns(s), :] - product(coefs[p, s], v_high[p], v_low[p], 1)

    with scope("g0"):
        gather_0(last)
        announce(0)
        load_x.wait()
        x_turned[...] = x_in[...].T
    with scope("g1"):
        gather_1(last)
        heard(0)
        announce(1)
    with scope("g3a"):
        gather_3(last, (0,))
    with scope("g2"):
        gather_2(last)
    with scope("g3"):
        gather_3(last, (1, 2, 3))
        gather_0(last - 1)
        heard(1)
    with scope("g4"):
        gather_4(last)
    with scope("prep"):
        prepare(last)
    for s in range(STREAMS):
        with scope("project"):
            project(last, s)
    for p in range(last, -1, -1):
        if p > 0:
            with scope("g1n"):
                gather_1(p - 1)
        for s in range(STREAMS):
            with scope(f"near{s}"):
                sum_near(p, s)
        if p > 0:
            with scope("g2n"):
                gather_2(p - 1)
            with scope("g3n"):
                gather_3(p - 1, range(4))
                if p > 1:
                    gather_0(p - 2)
        for s in range(STREAMS):
            with scope(f"far{s}"):
                sum_far(p, s)
        if p > 0:
            with scope("g4n"):
                gather_4(p - 1)
            with scope("prepn"):
                prepare(p - 1)
        for s in range(STREAMS):
            with scope(f"update{s}"):
                update(p, s)
            if p > 0:
                with scope("project"):
                    project(p - 1, s)
    with scope("out"):
        x_in[...] = x_turned[...].T
        store = pltpu.make_async_copy(x_in, out_ref, load_sem.at[0])
        store.start()
    with scope("drain"):
        for p in range(panels):
            whole = blocks.at[p, pl.ds(0, 15)]
            pltpu.make_async_remote_copy(
                src_ref=whole, dst_ref=whole, send_sem=gather_send.at[p], recv_sem=gather_last.at[p],
                device_id={"core": 1 - core}, device_id_type=MESH,
            ).wait_send()
        to_core(other_t, other_t, 0, factor_recv.at[0]).wait_send()
        whole_of(near, near_send.at[0], near_recv.at[0, 0]).wait_send()
        whole_of(far, far_send.at[0], far_recv.at[0, 0]).wait_send()
        whole_of(near, spread_send.at[0], spread_recv.at[0, 0]).wait_send()
        store.wait()


def per_device(vectors, reflectors, triangles):
    panels, rows, width = reflectors.shape
    length, count = vectors.shape
    turned = jnp.swapaxes(triangles, 1, 2)
    half = turned.shape[1] // 2
    part = count // STREAMS // 8
    f32, bf16 = jnp.float32, jnp.bfloat16
    dma = pltpu.SemaphoreType.DMA
    return pl.pallas_call(
        kernel,
        out_shape=jax.ShapeDtypeStruct(vectors.shape, f32),
        in_specs=[pl.BlockSpec(memory_space=pl.ANY)] * 3,
        out_specs=pl.BlockSpec(memory_space=pl.ANY),
        scratch_shapes=[
            pltpu.VMEM((length, count), f32),
            pltpu.VMEM((count, length), f32),
            pltpu.VMEM((panels, 16, rows + half, width), f32),
            pltpu.VMEM((panels, 16, half, width), f32),
            pltpu.VMEM((panels, 16 * rows, width), bf16),
            pltpu.VMEM((panels, 16 * rows, width), bf16),
            pltpu.VMEM((panels, width, width), bf16),
            pltpu.VMEM((panels, width, width), bf16),
            pltpu.VMEM((panels, STREAMS, 8 * part, width), f32),
            pltpu.VMEM((panels, STREAMS, 7, part, width), f32),
            pltpu.VMEM((panels, STREAMS, part, width), f32),
            pltpu.VMEM((panels, STREAMS, 3, part, width), f32),
            pltpu.VMEM((panels, STREAMS, 8 * part, width), f32),
            dma((2 * panels + 1,)), pltpu.SemaphoreType.REGULAR((2,)),
            dma((panels,)), dma((panels, 4)), dma((panels, 2)), dma((panels, 16)), dma((panels,)),
            dma((1,)), dma((panels,)), dma((1,)), dma((panels, STREAMS)),
            dma((1,)), dma((panels, STREAMS)), dma((1,)), dma((panels, STREAMS)),
        ],
        compiler_params=pltpu.CompilerParams(collective_id=0, has_side_effects=True),
    )(vectors, reflectors, turned)


def solution(mesh):
    finer = Mesh(mesh.devices.reshape(16, 2, 4, 4), ("z", "core", "y", "x"))
    placed = (P(ROW, VEC), P(None, ROW + VEC, None), P(None, None, VEC))
    return jax.shard_map(
        per_device, mesh=finer, in_specs=placed, out_specs=P(ROW, VEC), check_vma=False
    )
```

time: 312 us -> 97.2 us (0.31)
  blocking collectives: 151 us -> 0 us
  waiting for transfers between devices: 103 us -> 0 us
  Pallas kernels: 0 us -> 95.1 us
  matrix products: 25.9 us -> 0 us
  between operations: 13.5 us -> 0.01 us
  starting transfers between devices: 13.2 us -> 0 us
    all_to_all x5 -> x0, blocking collectives: 137 us -> none  [the longest x3 85.8 us: summed_on_arrival(): blocks = lax.all_to_all(cut_along(x, dim, count), axis, 0, 0, tiled=True)]
    pallas_call x0 -> x1, Pallas kernels: none -> 95.1 us  [per_device(): pl.pallas_call(kernel, out_shape=jax.ShapeDtypeStruct(vectors.shape, f32)...]
    all_gather x2 -> x0, waiting for transfers between devices: 79.9 us -> none  [the longest x1 69.4 us: per_device(): sections = lax.all_gather(reflectors, VEC, axis=1, tiled=True)]
    dot_general x9 -> x0, matrix products: 25.9 us -> none  [the longest x3 11.6 us: per_device(): jnp.dot(section, coefficients, precision=highest, preferred_element_type=...]
    all_to_all x1 -> x0, waiting for transfers between devices: 22 us -> none  [from_everyone(): lax.all_to_all(jnp.broadcast_to(x[None], (count, *x.shape)), axis, 0, 0,...]
    all_gather x1 -> x0, blocking collectives: 14 us -> none  [whole_of(): x = lax.all_gather(x, axis, axis=dim, tiled=True)]
    all_to_all x1 -> x0, starting transfers between devices: 13.2 us -> none  [from_everyone(): lax.all_to_all(jnp.broadcast_to(x[None], (count, *x.shape)), axis, 0, 0,...]
  transfers between devices with their start and end apart: 3 -> 0, of which waited for: 3 -> 0; matrix products, arithmetic and copies ran while one was open for 2% -> 0% of each run, Pallas kernels for 0% -> 0%
where the time goes in v2:
time: 97.2 us; the launch traced here: 97 us
  Pallas kernels  95.1 us (98%)
  local copies, waits for them, and re-layouts  1.87 us (2%)
    pallas_call x1, Pallas kernels, per_device(): pl.pallas_call(kernel, out_shape=jax.ShapeDtypeStruct(vectors.shape, f32)...  95.1 us

profile of v2, /device:TPU:1, one launch (start us, length us, event | category | flops | bytes accessed | tf_op | source)
XLA Modules:
  0.0 97.0 jit_solution(12735341466450102491)
XLA Ops:
  0.0 95.1 %shard_map.37 = f32[1024,128]{1,0:T(8,128)} custom-call(f32[1024,128]{1,0:T(8,128)} %x_ref.1, f32[3,64,512]{2,1,0:T(8,128)} %reflectors_ref.1, f32[3,32,512]{2,1,0:T(8,128)} %bitcast.1), custom_call_target="tpu_custom_call" | custom-call | tf_op jit(solution)/shard_map/pallas_call | solution.py:334
  95.1 1.9 %copy.5 = f32[1024,128]{1,0:T(8,128)} copy(f32[1024,128]{1,0:T(8,128)} %shard_map.37) | data formatting | bytes 1048576

commit v3 on v2

--- a/solution.py
+++ b/solution.py
@@ -13,7 +13,7 @@
 ROW = ("z", "core")
 STREAMS = 2
 
-SPANS = ((0, 40, 24), (40, 40, 16))
+CARRIED = ((0,), (1, 2), ())
 OFFSETS = (0, -1, 1, 2)
 
 
@@ -48,6 +48,9 @@
     me = y * 4 + x
     last = panels - 1
 
+    def length_of(p):
+        return rows + half_t * len(CARRIED[p])
+
     def scope(name):
         return jax.named_scope(name)
 
@@ -60,13 +63,14 @@
     loads = []
     for p in range(last, -1, -1):
         loads.append(pltpu.make_async_copy(reflectors_ref.at[p], blocks.at[p, me, pl.ds(0, rows), :], load_sem.at[2 * p]))
-        loads.append(
-            pltpu.make_async_copy(
-                factors_ref.at[p, pl.ds(pl.multiple_of(core * half_t, half_t), half_t), :],
-                blocks.at[p, me, pl.ds(rows, half_t), :],
-                load_sem.at[2 * p + 1],
+        for i, q in enumerate(CARRIED[p]):
+            loads.append(
+                pltpu.make_async_copy(
+                    factors_ref.at[q, pl.ds(pl.multiple_of(core * half_t, half_t), half_t), :],
+                    blocks.at[p, me, pl.ds(rows + i * half_t, half_t), :],
+                    load_sem.at[2 * q + 1],
+                )
             )
-        )
     load_x = pltpu.make_async_copy(x_ref, x_in, load_sem.at[2 * panels])
     for copy in loads:
         copy.start()
@@ -98,7 +102,8 @@
         return at["y"] * 4 + at["x"]
 
     def transfer(panel, half, recv, part, first, second, second_leg, by):
-        start, size, cut = SPANS[half]
+        size = length_of(panel) // 2
+        start, cut = half * size, (size // 2 + 7 * (1 - half)) // 8 * 8
         start, size = {"all": (start, size), "plus": (start, cut), "minus": (start + cut, size - cut)}[part]
         there = blocks.at[panel, block_at(half, first, second), pl.ds(start, size), :]
         axis = ("x", "y")[(half + second_leg) % 2]
@@ -155,7 +160,7 @@
                     final_leg(p, h, s, part, by).start()
 
     def gather_4(p):
-        whole = blocks.at[p, pl.ds(0, 4)]
+        whole = blocks.at[p, pl.ds(0, 4), pl.ds(0, length_of(p)), :]
         pltpu.make_async_remote_copy(
             src_ref=whole, dst_ref=whole, send_sem=gather_send.at[p], recv_sem=gather_last.at[p],
             device_id={"core": 1 - core}, device_id_type=MESH,
@@ -167,58 +172,86 @@
             device_id={"core": 1 - core}, device_id_type=MESH,
         )
 
-    def factor_copy(p):
-        return to_core(blocks.at[p, :, pl.ds(rows, half_t), :], other_t.at[p], 0, factor_recv.at[p])
+    def factor_copy(p, i, q):
+        here = blocks.at[p, :, pl.ds(rows + i * half_t, half_t), :]
+        return to_core(here, other_t.at[q], 0, factor_recv.at[q])
 
     def prepare(p):
-        factor_copy(p).start()
+        for i, q in enumerate(CARRIED[p]):
+            factor_copy(p, i, q).start()
 
         @pl.loop(0, 16)
         def _(b):
             at = pl.ds(pl.multiple_of(b * rows, rows), rows)
             v_high[p, at, :], v_low[p, at, :] = halves(blocks[p, b, 0:rows, :])
             at = pl.ds(pl.multiple_of(b * 32 + core * 16, 16), 16)
-            t_high[p, at, :], t_low[p, at, :] = halves(blocks[p, b, rows:, :])
-
-        factor_copy(p).wait_recv()
-
-        @pl.loop(0, 16)
-        def _(b):
-            at = pl.ds(pl.multiple_of(b * 32 + (1 - core) * 16, 16), 16)
-            t_high[p, at, :], t_low[p, at, :] = halves(other_t[p, b])
+            for i, q in enumerate(CARRIED[p]):
+                t_high[q, at, :], t_low[q, at, :] = halves(blocks[p, b, rows + i * half_t : rows + (i + 1) * half_t, :])
+
+        for i, q in enumerate(CARRIED[p]):
+            factor_copy(p, i, q).wait_recv()
+
+        if CARRIED[p]:
+
+            @pl.loop(0, 16)
+            def _(b):
+                at = pl.ds(pl.multiple_of(b * 32 + (1 - core) * 16, 16), 16)
+                for q in CARRIED[p]:
+                    t_high[q, at, :], t_low[q, at, :] = halves(other_t[q, b])
 
     count = x_turned.shape[0] // STREAMS
-    NEAR = ((0, 1), (1, 0), (1, 1), (-1, 0), (-1, 1), (2, 0), (2, 1))
-
-    def towards(s, by):
-        return by if s % 2 == 0 else -by
-
-    def part_of(chip, core_):
-        return pl.ds(pl.multiple_of((lax.rem(chip, 4) * 2 + core_) * (count // 8), count // 8), count // 8)
-
-    def near_copy(p, s, i):
-        by, flip = NEAR[i]
-        to, other = up(towards(s, by)), core + flip - 2 * core * flip
-        return pltpu.make_async_remote_copy(
-            src_ref=partial_c.at[p, s, part_of(to, other)], dst_ref=near.at[p, s, i],
+    part = count // 8
+
+    def first_of(quarter):
+        return quarter % 2 * 2 + quarter // 2 * 8
+
+    def chip_at(quarter, group, member):
+        return lax.rem(first_of(quarter) + group * 4 + member, depth)
+
+    def summing(group):
+        return 1 + group // 2
+
+    def group_of(quarter):
+        return lax.rem(z - first_of(quarter) + depth, depth) // 4
+
+    my_quarter = lax.rem(z + 3, 4) // 2 + lax.rem(z + 6 * (1 - lax.rem(z, 2)), depth) // 8 * 2
+    my_group = group_of(my_quarter)
+    my_member = summing(my_group)
+
+    def part_of(quarter, core_):
+        return pl.ds(pl.multiple_of((quarter * 2 + core_) * part, part), part)
+
+    def near_copy(p, s, by, other):
+        quarter = lax.rem(my_quarter + by, 4)
+        group = group_of(quarter)
+        member = lax.rem(z - first_of(quarter) + depth, 4)
+        return pltpu.make_async_remote_copy(
+            src_ref=partial_c.at[p, s, part_of(quarter, other)], dst_ref=near.at[p, s, member * 2 + core],
             send_sem=near_send.at[0], recv_sem=near_recv.at[p, s],
-            device_id={"z": to, "core": other}, device_id_type=MESH,
-        )
-
-    def far_copy(p, s, i):
-        return pltpu.make_async_remote_copy(
-            src_ref=near_sum.at[p, s], dst_ref=far.at[p, s, i],
+            device_id={"z": chip_at(quarter, group, summing(group)), "core": other}, device_id_type=MESH,
+        )
+
+    def far_copy(p, s, by):
+        group = lax.rem(my_group + by, 4)
+        return pltpu.make_async_remote_copy(
+            src_ref=near_sum.at[p, s], dst_ref=far.at[p, s, by - 1],
             send_sem=far_send.at[0], recv_sem=far_recv.at[p, s],
-            device_id={"z": up(4 * (i + 1))}, device_id_type=MESH,
-        )
-
-    def spread_copy(p, s, i):
-        by, flip = NEAR[i]
-        own = coefs.at[p, s, part_of(z, core)]
+            device_id={"z": chip_at(my_quarter, group, summing(group))}, device_id_type=MESH,
+        )
+
+    def spread_copy(p, s, by, other):
+        own = coefs.at[p, s, part_of(my_quarter, core)]
         return pltpu.make_async_remote_copy(
             src_ref=own, dst_ref=own, send_sem=spread_send.at[0], recv_sem=spread_recv.at[p, s],
-            device_id={"z": up(-towards(s, by)), "core": core + flip - 2 * core * flip}, device_id_type=MESH,
-        )
+            device_id={"z": chip_at(my_quarter, my_group, lax.rem(my_member + by, 4)), "core": other},
+            device_id_type=MESH,
+        )
+
+    def each_near(copy, p, s):
+        for by in (2, 1, 3):
+            copy(p, s, by, core).start()
+            copy(p, s, by, 1 - core).start()
+        copy(p, s, 0, 1 - core).start()
 
     def whole_of(ref, send, recv):
         return pltpu.make_async_remote_copy(
@@ -229,29 +262,26 @@
         return slice(s * count, (s + 1) * count)
 
     def project(p, s):
-        projected = product(x_turned[columns(s), :], v_high[p], v_low[p], 0)
-        partial_c[p, s] = product(projected, t_high[p], t_low[p], 0)
-        for i in (5, 6, 1, 2, 3, 4, 0):
-            near_copy(p, s, i).start()
+        partial_c[p, s] = product(x_turned[columns(s), :], v_high[p], v_low[p], 0)
+        each_near(near_copy, p, s)
 
     def sum_near(p, s):
-        whole_of(near.at[p, s], near_send.at[0], near_recv.at[p, s]).wait_recv()
-        total = partial_c[p, s, part_of(z, core)]
-        for i in range(7):
-            total = total + near[p, s, i]
-        near_sum[p, s] = total
-        for i in (1, 0, 2):
-            far_copy(p, s, i).start()
+        near[p, s, my_member * 2 + core] = partial_c[p, s, part_of(my_quarter, core)]
+        whole_of(near.at[p, s, pl.ds(0, 7)], near_send.at[0], near_recv.at[p, s]).wait_recv()
+        pairs = [near[p, s, i] + near[p, s, i + 1] for i in range(0, 8, 2)]
+        near_sum[p, s] = (pairs[0] + pairs[1]) + (pairs[2] + pairs[3])
+        for by in (2, 1, 3):
+            far_copy(p, s, by).start()
 
     def sum_far(p, s):
         whole_of(far.at[p, s], far_send.at[0], far_recv.at[p, s]).wait_recv()
-        coefs[p, s, part_of(z, core)] = (near_sum[p, s] + far[p, s, 1]) + (far[p, s, 0] + far[p, s, 2])
-        for i in (5, 6, 1, 2, 3, 4, 0):
-            spread_copy(p, s, i).start()
+        coefs[p, s, part_of(my_quarter, core)] = (near_sum[p, s] + far[p, s, 1]) + (far[p, s, 0] + far[p, s, 2])
+        each_near(spread_copy, p, s)
 
     def update(p, s):
-        whole_of(near.at[p, s], spread_send.at[0], spread_recv.at[p, s]).wait_recv()
-        x_turned[columns(s), :] = x_turned[columns(s), :] - product(coefs[p, s], v_high[p], v_low[p], 1)
+        whole_of(near.at[p, s, pl.ds(0, 7)], spread_send.at[0], spread_recv.at[p, s]).wait_recv()
+        scaled = product(coefs[p, s], t_high[p], t_low[p], 0)
+        x_turned[columns(s), :] = x_turned[columns(s), :] - product(scaled, v_high[p], v_low[p], 1)
 
     with scope("g0"):
         gather_0(last)
@@ -262,12 +292,10 @@
         gather_1(last)
         heard(0)
         announce(1)
-    with scope("g3a"):
-        gather_3(last, (0,))
     with scope("g2"):
         gather_2(last)
     with scope("g3"):
-        gather_3(last, (1, 2, 3))
+        gather_3(last, range(4))
         gather_0(last - 1)
         heard(1)
     with scope("g4"):
@@ -306,21 +334,18 @@
                 with scope("project"):
                     project(p - 1, s)
     with scope("out"):
-        x_in[...] = x_turned[...].T
-        store = pltpu.make_async_copy(x_in, out_ref, load_sem.at[0])
-        store.start()
+        out_ref[...] = x_turned[...].T
     with scope("drain"):
         for p in range(panels):
-            whole = blocks.at[p, pl.ds(0, 15)]
+            whole = blocks.at[p, pl.ds(0, 15), pl.ds(0, length_of(p)), :]
             pltpu.make_async_remote_copy(
                 src_ref=whole, dst_ref=whole, send_sem=gather_send.at[p], recv_sem=gather_last.at[p],
                 device_id={"core": 1 - core}, device_id_type=MESH,
             ).wait_send()
         to_core(other_t, other_t, 0, factor_recv.at[0]).wait_send()
-        whole_of(near, near_send.at[0], near_recv.at[0, 0]).wait_send()
+        whole_of(near.at[:, :, pl.ds(0, 7)], near_send.at[0], near_recv.at[0, 0]).wait_send()
         whole_of(far, far_send.at[0], far_recv.at[0, 0]).wait_send()
-        whole_of(near, spread_send.at[0], spread_recv.at[0, 0]).wait_send()
-        store.wait()
+        whole_of(near.at[:, :, pl.ds(0, 7)], spread_send.at[0], spread_recv.at[0, 0]).wait_send()
 
 
 def per_device(vectors, reflectors, triangles):
@@ -334,19 +359,19 @@
     return pl.pallas_call(
         kernel,
         out_shape=jax.ShapeDtypeStruct(vectors.shape, f32),
-        in_specs=[pl.BlockSpec(memory_space=pl.ANY)] * 3,
-        out_specs=pl.BlockSpec(memory_space=pl.ANY),
+        in_specs=[pl.BlockSpec(memory_space=pltpu.HBM)] * 3,
+        out_specs=pl.BlockSpec(memory_space=pltpu.VMEM),
         scratch_shapes=[
             pltpu.VMEM((length, count), f32),
             pltpu.VMEM((count, length), f32),
-            pltpu.VMEM((panels, 16, rows + half, width), f32),
+            pltpu.VMEM((panels, 16, rows + half * max(map(len, CARRIED)), width), f32),
             pltpu.VMEM((panels, 16, half, width), f32),
             pltpu.VMEM((panels, 16 * rows, width), bf16),
             pltpu.VMEM((panels, 16 * rows, width), bf16),
             pltpu.VMEM((panels, width, width), bf16),
             pltpu.VMEM((panels, width, width), bf16),
             pltpu.VMEM((panels, STREAMS, 8 * part, width), f32),
-            pltpu.VMEM((panels, STREAMS, 7, part, width), f32),
+            pltpu.VMEM((panels, STREAMS, 8, part, width), f32),
             pltpu.VMEM((panels, STREAMS, part, width), f32),
             pltpu.VMEM((panels, STREAMS, 3, part, width), f32),
             pltpu.VMEM((panels, STREAMS, 8 * part, width), f32),
@@ -355,8 +380,8 @@
             dma((1,)), dma((panels,)), dma((1,)), dma((panels, STREAMS)),
             dma((1,)), dma((panels, STREAMS)), dma((1,)), dma((panels, STREAMS)),
         ],
-        compiler_params=pltpu.CompilerParams(collective_id=0, has_side_effects=True),
-    )(vectors, reflectors, turned)
+        compiler_params=pltpu.CompilerParams(collective_id=0, has_side_effects=True, vmem_limit_bytes=36 * 2**20),
+    )(*(pltpu.with_memory_space_constraint(a, pltpu.HBM) for a in (vectors, reflectors, turned)))
 
 
 def solution(mesh):

time: 97.2 us -> 88.9 us (0.915)
  Pallas kernels: 95.1 us -> 88 us
  local copies, waits for them, and re-layouts: 1.87 us -> 0.8 us
    pallas_call x1, Pallas kernels: 95.1 us -> 88 us  [per_device(): pl.pallas_call(kernel, out_shape=jax.ShapeDtypeStruct(vectors.shape, f32)...]
    unnamed x1, local copies, waits for them, and re-layouts: 1.87 us -> 0.8 us
where the time goes in v3:
time: 88.9 us; the launch traced here: 88.8 us
  Pallas kernels  88 us (99%)
    pallas_call x1, Pallas kernels, per_device(): pl.pallas_call(kernel, out_shape=jax.ShapeDtypeStruct(vectors.shape, f32)...  88 us

profile of v3, /device:TPU:1, one launch (start us, length us, event | category | flops | bytes accessed | tf_op | source)
XLA Modules:
  0.0 88.8 jit_solution(4236469004317612395)
XLA Ops:
  0.0 88.0 %shard_map.37 = f32[1024,128]{1,0:T(8,128)S(1)} custom-call(f32[1024,128]{1,0:T(8,128)} %x_ref.1, f32[3,64,512]{2,1,0:T(8,128)} %reflectors_ref.1, f32[3,32,512]{2,1,0:T(8,128)} %bitcast.1), custom_call_target="tpu_custom_call" | custom-call | tf_op jit(solution)/shard_map/pallas_call | solution.py:359
  88.0 0.8 copy.5

commit v4 on v3

--- a/solution.py
+++ b/solution.py
@@ -12,8 +12,10 @@
 VEC = ("y", "x")
 ROW = ("z", "core")
 STREAMS = 2
-
-CARRIED = ((0,), (1, 2), ())
+SUMMING = 1
+
+CARRIED = (1, 2, None)
+ALONE = 0
 OFFSETS = (0, -1, 1, 2)
 
 
@@ -35,9 +37,9 @@
 
 def kernel(
     x_ref, reflectors_ref, factors_ref, out_ref,
-    x_in, x_turned, blocks, other_t, v_high, v_low, t_high, t_low, partial_c, near, near_sum, far, coefs,
+    x_in, x_turned, blocks, alone, other_t, v_high, v_low, t_high, t_low, partial_c, near, near_sum, far, coefs,
     load_sem, entered, gather_send, gather_first, gather_opposite, gather_second, gather_last,
-    core_send, factor_recv, near_send, near_recv, far_send, far_recv, spread_send, spread_recv,
+    alone_send, alone_recv, core_send, factor_recv, near_send, near_recv, far_send, far_recv, spread_send, spread_recv,
 ):
     panels, rows, width = reflectors_ref.shape
     half_t = factors_ref.shape[1] // 2
@@ -49,7 +51,7 @@
     last = panels - 1
 
     def length_of(p):
-        return rows + half_t * len(CARRIED[p])
+        return rows + half_t * (CARRIED[p] is not None)
 
     def scope(name):
         return jax.named_scope(name)
@@ -60,32 +62,31 @@
     def up(by):
         return lax.rem(z + by + depth, depth)
 
-    loads = []
-    for p in range(last, -1, -1):
-        loads.append(pltpu.make_async_copy(reflectors_ref.at[p], blocks.at[p, me, pl.ds(0, rows), :], load_sem.at[2 * p]))
-        for i, q in enumerate(CARRIED[p]):
-            loads.append(
-                pltpu.make_async_copy(
-                    factors_ref.at[q, pl.ds(pl.multiple_of(core * half_t, half_t), half_t), :],
-                    blocks.at[p, me, pl.ds(rows + i * half_t, half_t), :],
-                    load_sem.at[2 * q + 1],
-                )
-            )
-    load_x = pltpu.make_async_copy(x_ref, x_in, load_sem.at[2 * panels])
-    for copy in loads:
-        copy.start()
-    load_x.start()
-
+    def own_factor(q, there):
+        mine = pl.ds(pl.multiple_of(core * half_t, half_t), half_t)
+        return pltpu.make_async_copy(factors_ref.at[q, mine, :], there, load_sem.at[2 * q + 1])
+
+    def load(p):
+        copies = [pltpu.make_async_copy(reflectors_ref.at[p], blocks.at[p, me, pl.ds(0, rows), :], load_sem.at[2 * p])]
+        if CARRIED[p] is not None:
+            copies.append(own_factor(CARRIED[p], blocks.at[p, me, pl.ds(rows, half_t), :]))
+        if p == 0:
+            copies.append(own_factor(ALONE, alone.at[me]))
+        for copy in copies:
+            copy.start()
+        return copies
+
+    first_load = load(last)
     with scope("barrier"):
         barrier = pltpu.get_barrier_semaphore()
         for axis in ("x", "y"):
             for by in (1, -1):
                 pl.semaphore_signal(barrier, inc=1, device_id={axis: step(axis, by)}, device_id_type=MESH)
-        pl.semaphore_signal(barrier, inc=1, device_id={"core": 1 - core}, device_id_type=MESH)
-        for by in (1, -1, 2, -2):
+        for by in (2, -2, 1, -1):
             for other in (core, 1 - core):
                 pl.semaphore_signal(barrier, inc=1, device_id={"z": up(by), "core": other}, device_id_type=MESH)
-        for copy in loads:
+        pl.semaphore_signal(barrier, inc=1, device_id={"core": 1 - core}, device_id_type=MESH)
+        for copy in first_load:
             copy.wait()
         pl.semaphore_wait(barrier, 13)
 
@@ -152,8 +153,8 @@
             for by in (1, -1):
                 second_leg(p, h, 3, by).start()
 
-    def gather_3(p, which):
-        for s in which:
+    def gather_3(p):
+        for s in range(4):
             for h in (0, 1):
                 for by, part in ((1, "plus"), (-1, "minus")):
                     second_leg(p, h, s, by, -by).wait_recv()
@@ -172,35 +173,49 @@
             device_id={"core": 1 - core}, device_id_type=MESH,
         )
 
-    def factor_copy(p, i, q):
-        here = blocks.at[p, :, pl.ds(rows + i * half_t, half_t), :]
+    def factor_copy(q):
+        here = alone if q == ALONE else blocks.at[CARRIED.index(q), :, pl.ds(rows, half_t), :]
         return to_core(here, other_t.at[q], 0, factor_recv.at[q])
 
-    def prepare(p):
-        for i, q in enumerate(CARRIED[p]):
-            factor_copy(p, i, q).start()
-
+    def factor_rows(b, core_):
+        return pl.ds(pl.multiple_of(b * 32 + core_ * 16, 16), 16)
+
+    def split_panel(p):
         @pl.loop(0, 16)
         def _(b):
             at = pl.ds(pl.multiple_of(b * rows, rows), rows)
             v_high[p, at, :], v_low[p, at, :] = halves(blocks[p, b, 0:rows, :])
-            at = pl.ds(pl.multiple_of(b * 32 + core * 16, 16), 16)
-            for i, q in enumerate(CARRIED[p]):
-                t_high[q, at, :], t_low[q, at, :] = halves(blocks[p, b, rows + i * half_t : rows + (i + 1) * half_t, :])
-
-        for i, q in enumerate(CARRIED[p]):
-            factor_copy(p, i, q).wait_recv()
-
-        if CARRIED[p]:
-
-            @pl.loop(0, 16)
-            def _(b):
-                at = pl.ds(pl.multiple_of(b * 32 + (1 - core) * 16, 16), 16)
-                for q in CARRIED[p]:
-                    t_high[q, at, :], t_low[q, at, :] = halves(other_t[q, b])
+
+    def split_factor(q):
+        @pl.loop(0, 16)
+        def _(b):
+            mine = alone[b] if q == ALONE else blocks[CARRIED.index(q), b, rows : rows + half_t, :]
+            t_high[q, factor_rows(b, core), :], t_low[q, factor_rows(b, core), :] = halves(mine)
+
+        factor_copy(q).wait_recv()
+
+        @pl.loop(0, 16)
+        def _(b):
+            t_high[q, factor_rows(b, 1 - core), :], t_low[q, factor_rows(b, 1 - core), :] = halves(other_t[q, b])
+
+    def send_alone():
+        for dy in range(4):
+            for dx in range(4):
+                if dy or dx:
+                    pltpu.make_async_remote_copy(
+                        src_ref=alone.at[me], dst_ref=alone.at[me], send_sem=alone_send.at[0], recv_sem=alone_recv.at[0],
+                        device_id={"y": step("y", dy), "x": step("x", dx)}, device_id_type=MESH,
+                    ).start()
+
+    def alone_wait():
+        others = alone.at[pl.ds(0, 15)]
+        return pltpu.make_async_remote_copy(
+            src_ref=others, dst_ref=others, send_sem=alone_send.at[0], recv_sem=alone_recv.at[0],
+            device_id={"core": 1 - core}, device_id_type=MESH,
+        )
 
     count = x_turned.shape[0] // STREAMS
-    part = count // 8
+    part = count // 4
 
     def first_of(quarter):
         return quarter % 2 * 2 + quarter // 2 * 8
@@ -218,17 +233,17 @@
     my_group = group_of(my_quarter)
     my_member = summing(my_group)
 
-    def part_of(quarter, core_):
-        return pl.ds(pl.multiple_of((quarter * 2 + core_) * part, part), part)
-
-    def near_copy(p, s, by, other):
+    def part_of(quarter):
+        return pl.ds(pl.multiple_of(quarter * part, part), part)
+
+    def near_copy(p, s, by):
         quarter = lax.rem(my_quarter + by, 4)
         group = group_of(quarter)
         member = lax.rem(z - first_of(quarter) + depth, 4)
         return pltpu.make_async_remote_copy(
-            src_ref=partial_c.at[p, s, part_of(quarter, other)], dst_ref=near.at[p, s, member * 2 + core],
+            src_ref=partial_c.at[p, s, part_of(quarter)], dst_ref=near.at[p, s, member * 2 + core],
             send_sem=near_send.at[0], recv_sem=near_recv.at[p, s],
-            device_id={"z": chip_at(quarter, group, summing(group)), "core": other}, device_id_type=MESH,
+            device_id={"z": chip_at(quarter, group, summing(group)), "core": SUMMING}, device_id_type=MESH,
         )
 
     def far_copy(p, s, by):
@@ -236,23 +251,17 @@
         return pltpu.make_async_remote_copy(
             src_ref=near_sum.at[p, s], dst_ref=far.at[p, s, by - 1],
             send_sem=far_send.at[0], recv_sem=far_recv.at[p, s],
-            device_id={"z": chip_at(my_quarter, group, summing(group))}, device_id_type=MESH,
+            device_id={"z": chip_at(my_quarter, group, summing(group)), "core": SUMMING}, device_id_type=MESH,
         )
 
     def spread_copy(p, s, by, other):
-        own = coefs.at[p, s, part_of(my_quarter, core)]
+        own = coefs.at[p, s, part_of(my_quarter)]
         return pltpu.make_async_remote_copy(
             src_ref=own, dst_ref=own, send_sem=spread_send.at[0], recv_sem=spread_recv.at[p, s],
             device_id={"z": chip_at(my_quarter, my_group, lax.rem(my_member + by, 4)), "core": other},
             device_id_type=MESH,
         )
 
-    def each_near(copy, p, s):
-        for by in (2, 1, 3):
-            copy(p, s, by, core).start()
-            copy(p, s, by, 1 - core).start()
-        copy(p, s, 0, 1 - core).start()
-
     def whole_of(ref, send, recv):
         return pltpu.make_async_remote_copy(
             src_ref=ref, dst_ref=ref, send_sem=send, recv_sem=recv, device_id={"core": 1 - core}, device_id_type=MESH
@@ -263,29 +272,51 @@
 
     def project(p, s):
         partial_c[p, s] = product(x_turned[columns(s), :], v_high[p], v_low[p], 0)
-        each_near(near_copy, p, s)
+        for by in (2, 1, 3):
+            near_copy(p, s, by).start()
+
+        @pl.when(core != SUMMING)
+        def _():
+            near_copy(p, s, 0).start()
 
     def sum_near(p, s):
-        near[p, s, my_member * 2 + core] = partial_c[p, s, part_of(my_quarter, core)]
-        whole_of(near.at[p, s, pl.ds(0, 7)], near_send.at[0], near_recv.at[p, s]).wait_recv()
-        pairs = [near[p, s, i] + near[p, s, i + 1] for i in range(0, 8, 2)]
-        near_sum[p, s] = (pairs[0] + pairs[1]) + (pairs[2] + pairs[3])
-        for by in (2, 1, 3):
-            far_copy(p, s, by).start()
+        @pl.when(core == SUMMING)
+        def _():
+            near[p, s, my_member * 2 + SUMMING] = partial_c[p, s, part_of(my_quarter)]
+            whole_of(near.at[p, s, pl.ds(0, 7)], near_send.at[0], near_recv.at[p, s]).wait_recv()
+            pairs = [near[p, s, i] + near[p, s, i + 1] for i in range(0, 8, 2)]
+            near_sum[p, s] = (pairs[0] + pairs[1]) + (pairs[2] + pairs[3])
+            for by in (2, 1, 3):
+                far_copy(p, s, by).start()
 
     def sum_far(p, s):
-        whole_of(far.at[p, s], far_send.at[0], far_recv.at[p, s]).wait_recv()
-        coefs[p, s, part_of(my_quarter, core)] = (near_sum[p, s] + far[p, s, 1]) + (far[p, s, 0] + far[p, s, 2])
-        each_near(spread_copy, p, s)
+        @pl.when(core == SUMMING)
+        def _():
+            whole_of(far.at[p, s], far_send.at[0], far_recv.at[p, s]).wait_recv()
+            coefs[p, s, part_of(my_quarter)] = (near_sum[p, s] + far[p, s, 1]) + (far[p, s, 0] + far[p, s, 2])
+            for by in (2, 1, 3):
+                spread_copy(p, s, by, 1 - SUMMING).start()
+                spread_copy(p, s, by, SUMMING).start()
+            spread_copy(p, s, 0, 1 - SUMMING).start()
 
     def update(p, s):
-        whole_of(near.at[p, s, pl.ds(0, 7)], spread_send.at[0], spread_recv.at[p, s]).wait_recv()
+        @pl.when(core == SUMMING)
+        def _():
+            whole_of(near.at[p, s, pl.ds(0, 3)], spread_send.at[0], spread_recv.at[p, s]).wait_recv()
+
+        @pl.when(core != SUMMING)
+        def _():
+            whole_of(near.at[p, s, pl.ds(0, 4)], spread_send.at[0], spread_recv.at[p, s]).wait_recv()
+
         scaled = product(coefs[p, s], t_high[p], t_low[p], 0)
         x_turned[columns(s), :] = x_turned[columns(s), :] - product(scaled, v_high[p], v_low[p], 1)
 
     with scope("g0"):
         gather_0(last)
         announce(0)
+        load_x = pltpu.make_async_copy(x_ref, x_in, load_sem.at[2 * panels])
+        load_x.start()
+        later_loads = [copy for p in range(last - 1, -1, -1) for copy in load(p)]
         load_x.wait()
         x_turned[...] = x_in[...].T
     with scope("g1"):
@@ -295,20 +326,25 @@
     with scope("g2"):
         gather_2(last)
     with scope("g3"):
-        gather_3(last, range(4))
+        gather_3(last)
+        for copy in later_loads:
+            copy.wait()
         gather_0(last - 1)
         heard(1)
     with scope("g4"):
         gather_4(last)
     with scope("prep"):
-        prepare(last)
+        split_panel(last)
     for s in range(STREAMS):
         with scope("project"):
             project(last, s)
+    with scope("g1n"):
+        gather_1(last - 1)
     for p in range(last, -1, -1):
-        if p > 0:
-            with scope("g1n"):
-                gather_1(p - 1)
+        if p == 0:
+            with scope("alone"):
+                alone_wait().wait_recv()
+                factor_copy(ALONE).start()
         for s in range(STREAMS):
             with scope(f"near{s}"):
                 sum_near(p, s)
@@ -316,17 +352,25 @@
             with scope("g2n"):
                 gather_2(p - 1)
             with scope("g3n"):
-                gather_3(p - 1, range(4))
+                gather_3(p - 1)
                 if p > 1:
                     gather_0(p - 2)
+                else:
+                    send_alone()
         for s in range(STREAMS):
             with scope(f"far{s}"):
                 sum_far(p, s)
         if p > 0:
             with scope("g4n"):
                 gather_4(p - 1)
+                factor_copy(CARRIED[p - 1]).start()
             with scope("prepn"):
-                prepare(p - 1)
+                split_panel(p - 1)
+        if p > 1:
+            with scope("g1n"):
+                gather_1(p - 2)
+        with scope("factor"):
+            split_factor(p)
         for s in range(STREAMS):
             with scope(f"update{s}"):
                 update(p, s)
@@ -343,9 +387,16 @@
                 device_id={"core": 1 - core}, device_id_type=MESH,
             ).wait_send()
         to_core(other_t, other_t, 0, factor_recv.at[0]).wait_send()
-        whole_of(near.at[:, :, pl.ds(0, 7)], near_send.at[0], near_recv.at[0, 0]).wait_send()
-        whole_of(far, far_send.at[0], far_recv.at[0, 0]).wait_send()
-        whole_of(near.at[:, :, pl.ds(0, 7)], spread_send.at[0], spread_recv.at[0, 0]).wait_send()
+        alone_wait().wait_send()
+        @pl.when(core == SUMMING)
+        def _():
+            whole_of(near.at[:, :, pl.ds(0, 3)], near_send.at[0], near_recv.at[0, 0]).wait_send()
+            whole_of(far, far_send.at[0], far_recv.at[0, 0]).wait_send()
+            whole_of(near.at[:, :, pl.ds(0, 7)], spread_send.at[0], spread_recv.at[0, 0]).wait_send()
+
+        @pl.when(core != SUMMING)
+        def _():
+            whole_of(near.at[:, :, pl.ds(0, 4)], near_send.at[0], near_recv.at[0, 0]).wait_send()
 
 
 def per_device(vectors, reflectors, triangles):
@@ -353,7 +404,7 @@
     length, count = vectors.shape
     turned = jnp.swapaxes(triangles, 1, 2)
     half = turned.shape[1] // 2
-    part = count // STREAMS // 8
+    part = count // STREAMS // 4
     f32, bf16 = jnp.float32, jnp.bfloat16
     dma = pltpu.SemaphoreType.DMA
     return pl.pallas_call(
@@ -364,20 +415,21 @@
         scratch_shapes=[
             pltpu.VMEM((length, count), f32),
             pltpu.VMEM((count, length), f32),
-            pltpu.VMEM((panels, 16, rows + half * max(map(len, CARRIED)), width), f32),
+            pltpu.VMEM((panels, 16, rows + half, width), f32),
+            pltpu.VMEM((16, half, width), f32),
             pltpu.VMEM((panels, 16, half, width), f32),
             pltpu.VMEM((panels, 16 * rows, width), bf16),
             pltpu.VMEM((panels, 16 * rows, width), bf16),
             pltpu.VMEM((panels, width, width), bf16),
             pltpu.VMEM((panels, width, width), bf16),
-            pltpu.VMEM((panels, STREAMS, 8 * part, width), f32),
+            pltpu.VMEM((panels, STREAMS, 4 * part, width), f32),
             pltpu.VMEM((panels, STREAMS, 8, part, width), f32),
             pltpu.VMEM((panels, STREAMS, part, width), f32),
             pltpu.VMEM((panels, STREAMS, 3, part, width), f32),
-            pltpu.VMEM((panels, STREAMS, 8 * part, width), f32),
+            pltpu.VMEM((panels, STREAMS, 4 * part, width), f32),
             dma((2 * panels + 1,)), pltpu.SemaphoreType.REGULAR((2,)),
             dma((panels,)), dma((panels, 4)), dma((panels, 2)), dma((panels, 16)), dma((panels,)),
-            dma((1,)), dma((panels,)), dma((1,)), dma((panels, STREAMS)),
+            dma((1,)), dma((1,)), dma((1,)), dma((panels,)), dma((1,)), dma((panels, STREAMS)),
             dma((1,)), dma((panels, STREAMS)), dma((1,)), dma((panels, STREAMS)),
         ],
         compiler_params=pltpu.CompilerParams(collective_id=0, has_side_effects=True, vmem_limit_bytes=36 * 2**20),

time: 88.9 us -> 85.5 us (0.962)
  Pallas kernels: 88 us -> 83.7 us
    pallas_call x1, Pallas kernels: 88 us -> 83.7 us  [per_device(): pl.pallas_call(kernel, out_shape=jax.ShapeDtypeStruct(vectors.shape, f32)...]
where the time goes in v4:
time: 85.5 us; the launch traced here: 84.5 us
  Pallas kernels  83.7 us (98%)
    pallas_call x1, Pallas kernels, per_device(): pl.pallas_call(kernel, out_shape=jax.ShapeDtypeStruct(vectors.shape, f32)...  83.7 us

profile of v4, /device:TPU:1, one launch (start us, length us, event | category | flops | bytes accessed | tf_op | source)
XLA Modules:
  0.0 84.5 jit_solution(13360543129722148980)
XLA Ops:
  0.0 83.7 %shard_map.37 = f32[1024,128]{1,0:T(8,128)S(1)} custom-call(f32[1024,128]{1,0:T(8,128)} %x_ref.1, f32[3,64,512]{2,1,0:T(8,128)} %reflectors_ref.1, f32[3,32,512]{2,1,0:T(8,128)} %bitcast.1), custom_call_target="tpu_custom_call" | custom-call | tf_op jit(solution)/shard_map/pallas_call | solution.py:410
  83.7 0.8 copy.5

commit v5 on v4

--- a/solution.py
+++ b/solution.py
@@ -37,7 +37,7 @@
 
 def kernel(
     x_ref, reflectors_ref, factors_ref, out_ref,
-    x_in, x_turned, blocks, alone, other_t, v_high, v_low, t_high, t_low, partial_c, near, near_sum, far, coefs,
+    x_in, x_turned, blocks, alone, other_t, v_high, v_low, w_high, w_low, t_high, t_low, partial_c, near, near_sum, far, coefs,
     load_sem, entered, gather_send, gather_first, gather_opposite, gather_second, gather_last,
     alone_send, alone_recv, core_send, factor_recv, near_send, near_recv, far_send, far_recv, spread_send, spread_recv,
 ):
@@ -80,22 +80,25 @@
     with scope("barrier"):
         barrier = pltpu.get_barrier_semaphore()
         for axis in ("x", "y"):
-            for by in (1, -1):
+            for by in (1, -1, 2):
                 pl.semaphore_signal(barrier, inc=1, device_id={axis: step(axis, by)}, device_id_type=MESH)
-        for by in (2, -2, 1, -1):
+        for by in (1, -1):
             for other in (core, 1 - core):
                 pl.semaphore_signal(barrier, inc=1, device_id={"z": up(by), "core": other}, device_id_type=MESH)
         pl.semaphore_signal(barrier, inc=1, device_id={"core": 1 - core}, device_id_type=MESH)
         for copy in first_load:
             copy.wait()
-        pl.semaphore_wait(barrier, 13)
+        pl.semaphore_wait(barrier, 11)
 
     def announce(round_):
         for by in (1, -1):
-            pl.semaphore_signal(entered.at[round_], inc=1, device_id={"z": up(by * 2 * 2**round_)}, device_id_type=MESH)
+            to = up(by * (1, 2, 4)[round_])
+            pl.semaphore_signal(entered.at[round_], inc=1, device_id={"z": to}, device_id_type=MESH)
+            if round_ == 0:
+                pl.semaphore_signal(entered.at[0], inc=1, device_id={"z": to, "core": 1 - core}, device_id_type=MESH)
 
     def heard(round_):
-        pl.semaphore_wait(entered.at[round_], 2)
+        pl.semaphore_wait(entered.at[round_], 4 if round_ == 0 else 2)
 
     def block_at(half, first, second):
         first_axis, second_axis = ("x", "y") if half == 0 else ("y", "x")
@@ -122,6 +125,9 @@
     def opposite(p, h, part, by, first):
         return transfer(p, h, gather_opposite.at[p, h], part, first, 0, 0, by)
 
+    def straight(p, h):
+        return transfer(p, h, gather_opposite.at[p, h], "all", 0, 0, 0, 2)
+
     def second_leg(p, h, s, by, second=0):
         return transfer(p, h, gather_second.at[p, (h * 4 + s) * 2 + side(by)], "all", OFFSETS[s], second, 1, by)
 
@@ -132,6 +138,12 @@
         for h in (0, 1):
             for by in (1, -1):
                 first_leg(p, h, by).start()
+
+        @pl.when(core != SUMMING)
+        def _():
+            for h in (0, 1):
+                straight(p, h).start()
+
         for h in (0, 1):
             for by in (1, -1):
                 second_leg(p, h, 0, by).start()
@@ -139,9 +151,13 @@
     def gather_1(p):
         for h in (0, 1):
             first_leg(p, h, 1, -1).wait_recv()
-            opposite(p, h, "plus", 1, -1).start()
             first_leg(p, h, -1, 1).wait_recv()
-            opposite(p, h, "minus", -1, 1).start()
+
+            @pl.when(core == SUMMING)
+            def _():
+                opposite(p, h, "plus", 1, -1).start()
+                opposite(p, h, "minus", -1, 1).start()
+
         for h in (0, 1):
             for s in (1, 2):
                 for by in (1, -1):
@@ -185,6 +201,13 @@
         def _(b):
             at = pl.ds(pl.multiple_of(b * rows, rows), rows)
             v_high[p, at, :], v_low[p, at, :] = halves(blocks[p, b, 0:rows, :])
+
+    def turn_panel(p):
+        @pl.loop(0, 8)
+        def _(i):
+            at = pl.ds(pl.multiple_of(i * 2 * rows, 2 * rows), 2 * rows)
+            two = jnp.concatenate([blocks[p, 2 * i, 0:rows, :], blocks[p, 2 * i + 1, 0:rows, :]], axis=0)
+            w_high[p, :, at], w_low[p, :, at] = halves(two.T)
 
     def split_factor(q):
         @pl.loop(0, 16)
@@ -309,7 +332,7 @@
             whole_of(near.at[p, s, pl.ds(0, 4)], spread_send.at[0], spread_recv.at[p, s]).wait_recv()
 
         scaled = product(coefs[p, s], t_high[p], t_low[p], 0)
-        x_turned[columns(s), :] = x_turned[columns(s), :] - product(scaled, v_high[p], v_low[p], 1)
+        x_turned[columns(s), :] = x_turned[columns(s), :] - product(scaled, w_high[p], w_low[p], 0)
 
     with scope("g0"):
         gather_0(last)
@@ -325,14 +348,16 @@
         announce(1)
     with scope("g2"):
         gather_2(last)
+        heard(1)
+        announce(2)
     with scope("g3"):
         gather_3(last)
         for copy in later_loads:
             copy.wait()
         gather_0(last - 1)
-        heard(1)
     with scope("g4"):
         gather_4(last)
+        heard(2)
     with scope("prep"):
         split_panel(last)
     for s in range(STREAMS):
@@ -345,6 +370,8 @@
             with scope("alone"):
                 alone_wait().wait_recv()
                 factor_copy(ALONE).start()
+        with scope("turn"):
+            turn_panel(p)
         for s in range(STREAMS):
             with scope(f"near{s}"):
                 sum_near(p, s)
@@ -420,6 +447,8 @@
             pltpu.VMEM((panels, 16, half, width), f32),
             pltpu.VMEM((panels, 16 * rows, width), bf16),
             pltpu.VMEM((panels, 16 * rows, width), bf16),
+            pltpu.VMEM((panels, width, 16 * rows), bf16),
+            pltpu.VMEM((panels, width, 16 * rows), bf16),
             pltpu.VMEM((panels, width, width), bf16),
             pltpu.VMEM((panels, width, width), bf16),
             pltpu.VMEM((panels, STREAMS, 4 * part, width), f32),
@@ -427,7 +456,7 @@
             pltpu.VMEM((panels, STREAMS, part, width), f32),
             pltpu.VMEM((panels, STREAMS, 3, part, width), f32),
             pltpu.VMEM((panels, STREAMS, 4 * part, width), f32),
-            dma((2 * panels + 1,)), pltpu.SemaphoreType.REGULAR((2,)),
+            dma((2 * panels + 1,)), pltpu.SemaphoreType.REGULAR((3,)),
             dma((panels,)), dma((panels, 4)), dma((panels, 2)), dma((panels, 16)), dma((panels,)),
             dma((1,)), dma((1,)), dma((1,)), dma((panels,)), dma((1,)), dma((panels, STREAMS)),
             dma((1,)), dma((panels, STREAMS)), dma((1,)), dma((panels, STREAMS)),

time: 85.5 us -> 85.2 us (level)
  no operation moved by 1% of the time
where the time goes in v5:
time: 85.2 us; the launch traced here: 85 us
  Pallas kernels  84.2 us (99%)
    pallas_call x1, Pallas kernels, per_device(): pl.pallas_call(kernel, out_shape=jax.ShapeDtypeStruct(vectors.shape, f32)...  84.2 us

profile of v5, /device:TPU:1, one launch (start us, length us, event | category | flops | bytes accessed | tf_op | source)
XLA Modules:
  0.0 85.0 jit_solution(10658597153250659394)
XLA Ops:
  0.0 84.2 %shard_map.37 = f32[1024,128]{1,0:T(8,128)S(1)} custom-call(f32[1024,128]{1,0:T(8,128)} %x_ref.1, f32[3,64,512]{2,1,0:T(8,128)} %reflectors_ref.1, f32[3,32,512]{2,1,0:T(8,128)} %bitcast.1), custom_call_target="tpu_custom_call" | custom-call | tf_op jit(solution)/shard_map/pallas_call | solution.py:437
  84.2 0.8 copy.5

commit v6 on v5

--- a/solution.py
+++ b/solution.py
@@ -372,12 +372,16 @@
                 factor_copy(ALONE).start()
         with scope("turn"):
             turn_panel(p)
+        if p == 1:
+            with scope("g2n"):
+                gather_2(p - 1)
         for s in range(STREAMS):
             with scope(f"near{s}"):
                 sum_near(p, s)
         if p > 0:
-            with scope("g2n"):
-                gather_2(p - 1)
+            if p > 1:
+                with scope("g2n"):
+                    gather_2(p - 1)
             with scope("g3n"):
                 gather_3(p - 1)
                 if p > 1:

time: 85.2 us -> 81.7 us (0.959)
  Pallas kernels: 84.2 us -> 80.1 us
    pallas_call x1, Pallas kernels: 84.2 us -> 80.1 us  [per_device(): pl.pallas_call(kernel, out_shape=jax.ShapeDtypeStruct(vectors.shape, f32)...]
where the time goes in v6:
time: 81.7 us; the launch traced here: 80.9 us
  Pallas kernels  80.1 us (98%)
    pallas_call x1, Pallas kernels, per_device(): pl.pallas_call(kernel, out_shape=jax.ShapeDtypeStruct(vectors.shape, f32)...  80.1 us

profile of v6, /device:TPU:1, one launch (start us, length us, event | category | flops | bytes accessed | tf_op | source)
XLA Modules:
  0.0 80.9 jit_solution(7506629295974201662)
XLA Ops:
  0.0 80.1 %shard_map.37 = f32[1024,128]{1,0:T(8,128)S(1)} custom-call(f32[1024,128]{1,0:T(8,128)} %x_ref.1, f32[3,64,512]{2,1,0:T(8,128)} %reflectors_ref.1, f32[3,32,512]{2,1,0:T(8,128)} %bitcast.1), custom_call_target="tpu_custom_call" | custom-call | tf_op jit(solution)/shard_map/pallas_call | solution.py:441
  80.2 0.8 copy.5

commit v7 on v6

--- a/solution.py
+++ b/solution.py
@@ -370,14 +370,18 @@
             with scope("alone"):
                 alone_wait().wait_recv()
                 factor_copy(ALONE).start()
-        with scope("turn"):
-            turn_panel(p)
+        if p > 0:
+            with scope("turn"):
+                turn_panel(p)
         if p == 1:
             with scope("g2n"):
                 gather_2(p - 1)
         for s in range(STREAMS):
             with scope(f"near{s}"):
                 sum_near(p, s)
+        if p == 0:
+            with scope("turn"):
+                turn_panel(p)
         if p > 0:
             if p > 1:
                 with scope("g2n"):

time: 81.7 us -> 81.7 us (level)
  no operation moved by 1% of the time
where the time goes in v7:
time: 81.7 us; the launch traced here: 80.9 us
  Pallas kernels  80.1 us (98%)
    pallas_call x1, Pallas kernels, per_device(): pl.pallas_call(kernel, out_shape=jax.ShapeDtypeStruct(vectors.shape, f32)...  80.1 us

profile of v7, /device:TPU:1, one launch (start us, length us, event | category | flops | bytes accessed | tf_op | source)
XLA Modules:
  0.0 80.9 jit_solution(11693637656358698837)
XLA Ops:
  0.0 80.1 %shard_map.37 = f32[1024,128]{1,0:T(8,128)S(1)} custom-call(f32[1024,128]{1,0:T(8,128)} %x_ref.1, f32[3,64,512]{2,1,0:T(8,128)} %reflectors_ref.1, f32[3,32,512]{2,1,0:T(8,128)} %bitcast.1), custom_call_target="tpu_custom_call" | custom-call | tf_op jit(solution)/shard_map/pallas_call | solution.py:445
  80.2 0.8 copy.5
